TPU v7x, 256 devices: a whole 4x4x8 slice. The times are simulated.
256 devices in a mesh: ctx: 16 (over z_hi, x), tp: 4 (over y), dp: 4 (over z_lo, core).
Axes of the slice: x: 4, y: 4, z: 8 (z_hi: 4, z_lo: 2; z = z_hi * 2 + z_lo), core: 2. Of those that a mesh axis runs over, the one named last changes fastest.
Arguments:
- byte_embed: bfloat16 [65536, 1024], P(('dp', 'ctx', 'tp')), parts along dimension 0, may hold values from -6 to 6
- patch_start: int32 [65536], P(('dp', 'ctx', 'tp')), parts along dimension 0, may hold values from 0 to 1, as said below
- enc_gain: float32 [1024], replicated, may hold values from 0.1 to 1.9
- enc_qkv: bfloat16 [1024, 3072], replicated, may hold values from -4 to 4
- enc_out: bfloat16 [1024, 1024], replicated, may hold values from -0.1875 to 0.1875
- up_proj: bfloat16 [1024, 4096], P('ctx', 'tp'), may hold values from -0.1875 to 0.1875
- lat_gain: float32 [4096], replicated, may hold values from 0.1 to 1.9
- query_proj: bfloat16 [4096, 2048], P('ctx', 'tp'), may hold values from -4 to 4
- key_proj: bfloat16 [4096, 512], P('ctx', 'tp'), may hold values from -4 to 4
- value_matrix: bfloat16 [4096, 512], P('ctx', 'tp'), may hold values from -0.09375 to 0.09375
- out_proj: bfloat16 [2048, 4096], P('tp', 'ctx'), may hold values from -0.125 to 0.125
- down_proj: bfloat16 [4096, 1024], P('tp', 'ctx'), may hold values from -0.09375 to 0.09375
Outputs:
- byte_states: bfloat16 [65536, 1024], P(('dp', 'ctx', 'tp')), parts along dimension 0
There are 4 independent parts, one for each index of `dp`. A program takes and returns all parts, laid end to end along the dimension named above; an argument that names none is the same for every part. Nothing has to cross between parts.
Inputs may be any that keep to these rules, and one draw needn't show every extreme that they name: `patch_start`: byte 0 begins a patch; every patch spans 1 to 19 bytes; each aligned group of 1024 bytes holds at most 256 patch starts, and some group holds exactly 256.
All inputs are finite; a program needn't handle non-finite values.
Results may differ from a plain program's by a relative error of at most 0.015.
Values may be sent and summed in bfloat16 or wider, within the bound.
A program may use at most 128 MiB of HBM per device.

v0:
```python
import jax
import jax.numpy as jnp
from jax import lax
from jax.sharding import PartitionSpec as P

BH = 16
HB = 64
HEAD_SIZE = 128
WIN = 512
EPS = 1e-05


def shifted(block, axis, distance):
    devices = range(lax.axis_size(axis))
    route = [(i - distance, i) for i in devices if i - distance in devices]
    return lax.ppermute(block, axis, route)


def in_order(parts, dim):
    parts = jnp.moveaxis(parts, 0, dim)
    dims = parts.shape
    return parts.reshape(*dims[:dim], dims[dim] * dims[dim + 1], *dims[dim + 2 :])


def from_everyone(value, axis):
    copies = jnp.broadcast_to(value, (lax.axis_size(axis), *value.shape))
    return lax.all_to_all(copies, axis, split_axis=0, concat_axis=0, tiled=True)


def gathered_copies(value, axis, dim):
    return in_order(from_everyone(value, axis), dim)


def in_blocks(value, dim, peers):
    before, after = (value.shape[:dim], value.shape[dim + 1 :])
    return jnp.moveaxis(value.reshape(*before, peers, -1, *after), dim, 0)


def sum_at_owner(value, axis, dim):
    parts = in_blocks(value, dim, lax.axis_size(axis))
    arrived = lax.all_to_all(parts, axis, split_axis=0, concat_axis=0, tiled=True)
    return arrived.astype(jnp.float32).sum(axis=0)


def in_one_piece(arrays, axis, dim, along):
    columns = [a.reshape(*a.shape[:along], -1) for a in arrays]
    both = jnp.concatenate(columns, axis=along)
    result, at, gathered = (sum_at_owner(both, axis, dim), 0, [])
    for a, column in zip(arrays, columns):
        piece = result[..., at : at + column.shape[along]]
        gathered.append(piece.reshape(*piece.shape[:along], *a.shape[along:]))
        at += column.shape[along]
    return tuple(gathered)


def sent_together(arrays, axis, dim, along):
    ends, at = ([], 0)
    for a in arrays[:-1]:
        at += a.shape[along]
        ends.append(at)
    both = jnp.concatenate(arrays, axis=along)
    return tuple(jnp.split(lax.all_gather(both, axis, axis=dim, tiled=True), ends, axis=along))


def taken_together(value, axis):
    everything = from_everyone(value, axis)
    return jnp.sum(everything.astype(jnp.float32), axis=0)


def rms_scale(values, gain):
    floats = values.astype(jnp.float32)
    return floats * lax.rsqrt(jnp.mean(floats * floats, axis=-1, keepdims=True) + EPS) * gain


def window_attend(query, keys, values, first):
    n_query = query.shape[0]
    n_key = keys.shape[0]
    qh = query.reshape(n_query, BH, HB)
    kh = keys.reshape(n_key, BH, HB)
    vh = values.reshape(n_key, BH, HB)
    scores = jnp.einsum("qhd,khd->hqk", qh, kh, preferred_element_type=jnp.float32) / jnp.sqrt(
        jnp.float32(HB)
    )
    q_pos = first + jnp.arange(n_query, dtype=jnp.int32)
    k_pos = first - (n_key - n_query) + jnp.arange(n_key, dtype=jnp.int32)
    allowed = (
        (k_pos[None, :] <= q_pos[:, None])
        & (k_pos[None, :] > q_pos[:, None] - WIN)
        & (k_pos[None, :] >= 0)
    )
    scores = jnp.where(allowed[None], scores, jnp.float32(-1e30))
    peak = jnp.max(scores, axis=-1, keepdims=True)
    expo = jnp.where(allowed[None], jnp.exp(scores - peak), jnp.float32(0.0))
    total = jnp.sum(expo, axis=-1, keepdims=True)
    mixed = (
        jnp.einsum(
            "hqk,khd->hqd", expo.astype(jnp.bfloat16), vh, preferred_element_type=jnp.float32
        )
        / total
    )
    return jnp.transpose(mixed, (1, 0, 2)).reshape(n_query, BH * HB).astype(jnp.bfloat16)


def local(
    byte_embed,
    patch_start,
    enc_gain,
    enc_qkv,
    enc_out,
    up_proj,
    lat_gain,
    query_proj,
    key_proj,
    value_matrix,
    out_proj,
    down_proj,
):
    nbytes = byte_embed.shape[0]
    width = byte_embed.shape[1]
    n_tp = lax.axis_size("tp")
    n_ctx = lax.axis_size("ctx")
    device = lax.axis_index(("ctx", "tp"))
    group = device // n_tp
    slots = n_tp * nbytes // 4
    normed = rms_scale(byte_embed, enc_gain).astype(jnp.bfloat16)
    qkv = jnp.dot(normed, enc_qkv, preferred_element_type=jnp.float32).astype(jnp.bfloat16)
    query = qkv[:, :width]
    earlier = (qkv[:, width : 2 * width], qkv[:, 2 * width :])
    key_list = [earlier[0]]
    value_list = [earlier[1]]
    for step in range(2):
        earlier = shifted((earlier[0], earlier[1]), ("ctx", "tp"), 1)
        key_list.insert(0, earlier[0])
        value_list.insert(0, earlier[1])
    context = window_attend(
        query,
        jnp.concatenate(key_list, axis=0),
        jnp.concatenate(value_list, axis=0),
        device * nbytes,
    )
    hidden = (
        byte_embed.astype(jnp.float32)
        + jnp.dot(context, enc_out, preferred_element_type=jnp.float32)
    ).astype(jnp.bfloat16)
    local_count = jnp.sum(patch_start)
    all_counts = gathered_copies(local_count[None], ("ctx", "tp"), 0)
    before = jnp.cumsum(all_counts) - all_counts
    offset = before[device] - before[group * n_tp]
    group_counts = jnp.sum(all_counts.reshape(n_ctx, n_tp), axis=1)
    local_slot = jnp.cumsum(patch_start) - 1
    slot = offset + local_slot
    columns = jnp.arange(slots, dtype=jnp.int32)
    onehot = ((slot[:, None] == columns[None, :]) & (local_slot[:, None] >= 0)).astype(jnp.bfloat16)
    part_sum = jnp.dot(onehot.T, hidden, preferred_element_type=jnp.float32)
    part_count = jnp.sum(onehot.astype(jnp.float32), axis=0)
    leading = (local_slot < 0).astype(jnp.bfloat16)
    lead_sum = jnp.dot(leading[None, :], hidden, preferred_element_type=jnp.float32)
    lead_count = jnp.sum(leading.astype(jnp.float32))[None]
    recv_sum, recv_count = shifted((lead_sum, lead_count), ("ctx", "tp"), -1)
    last = offset + local_count - 1
    last_hot = (columns == last).astype(jnp.float32)
    part_sum = part_sum + last_hot[:, None] * recv_sum
    part_count = part_count + last_hot * recv_count
    sums, counts = in_one_piece(
        (part_sum.astype(jnp.bfloat16), part_count.astype(jnp.bfloat16)), "tp", 0, 1
    )
    share = (sums / jnp.maximum(counts, 1.0)[:, None]).astype(jnp.bfloat16)
    pooled = gathered_copies(share, "tp", 0)
    latent_part = jnp.dot(
        pooled,
        lax.all_gather(up_proj, "ctx", axis=0, tiled=True),
        preferred_element_type=jnp.float32,
    ).astype(jnp.bfloat16)
    latent = gathered_copies(latent_part, "tp", 1)
    lnorm = rms_scale(latent, lat_gain).astype(jnp.bfloat16)

    def proj_add(piece):
        return jnp.dot(lnorm, piece, preferred_element_type=jnp.float32)

    pieces = sent_together((query_proj, key_proj, value_matrix), "ctx", 0, 1)
    q_sum, k_sum, v_sum = tuple((proj_add(pieces[i]) for i in range(3)))
    q_local = q_sum.astype(jnp.bfloat16)
    k_local = k_sum.astype(jnp.bfloat16)
    v_local = v_sum.astype(jnp.bfloat16)
    heads_local = q_local.shape[1] // HEAD_SIZE
    kv_local = k_local.shape[1] // HEAD_SIZE
    share_count = heads_local // kv_local
    q_grouped = jnp.transpose(
        q_local.reshape(slots, kv_local, share_count, HEAD_SIZE), (1, 2, 0, 3)
    ).reshape(kv_local, share_count * slots, HEAD_SIZE)
    query_rows = group * slots + jnp.tile(jnp.arange(slots, dtype=jnp.int32), share_count)
    scale = 1.0 / jnp.sqrt(jnp.float32(HEAD_SIZE))
    peak = jnp.full((kv_local, share_count * slots), -1e30, jnp.float32)
    k_piece, v_piece = sent_together((k_local, v_local), "ctx", 0, 1)
    count = k_piece.shape[0]
    k_heads = jnp.transpose(k_piece.reshape(count, kv_local, HEAD_SIZE), (1, 0, 2))
    v_heads = jnp.transpose(v_piece.reshape(count, kv_local, HEAD_SIZE), (1, 0, 2))
    key_rows = jnp.arange(count, dtype=jnp.int32)
    used = key_rows % slots < group_counts[key_rows // slots]
    allowed = used[None, :] & (key_rows[None, :] <= query_rows[:, None])
    scores = (
        jnp.einsum("hqd,hkd->hqk", q_grouped, k_heads, preferred_element_type=jnp.float32) * scale
    )
    scores = jnp.where(allowed[None], scores, jnp.float32(-1e30))
    new_peak = jnp.maximum(peak, jnp.max(scores, axis=-1))
    expo = jnp.where(allowed[None], jnp.exp(scores - new_peak[..., None]), jnp.float32(0.0))
    total = jnp.sum(expo, axis=-1)
    accum = jnp.einsum(
        "hqk,hkd->hqd", expo.astype(jnp.bfloat16), v_heads, preferred_element_type=jnp.float32
    )
    peak, total, accum = (new_peak, total, accum)
    mixed = accum / total[..., None]
    attn = (
        jnp.transpose(mixed.reshape(kv_local, share_count, slots, HEAD_SIZE), (2, 0, 1, 3))
        .reshape(slots, heads_local * HEAD_SIZE)
        .astype(jnp.bfloat16)
    )
    partial_value = jnp.dot(
        attn,
        lax.all_gather(out_proj, "ctx", axis=1, tiled=True),
        preferred_element_type=jnp.float32,
    )
    attn_part = sum_at_owner(partial_value.astype(jnp.bfloat16), "tp", 1)
    latent_out = (latent_part.astype(jnp.float32) + attn_part).astype(jnp.bfloat16)
    down_part = jnp.dot(
        latent_out,
        lax.all_gather(down_proj, "ctx", axis=1, tiled=True),
        preferred_element_type=jnp.float32,
    )
    patch_out = (
        taken_together(down_part.astype(jnp.bfloat16), "tp")
        .astype(jnp.float32)
        .astype(jnp.bfloat16)
    )
    trailing = lax.dynamic_slice_in_dim(patch_out, last, 1, 0)
    carried = shifted(trailing, ("ctx", "tp"), 1)
    spread = jnp.dot(onehot, patch_out, preferred_element_type=jnp.float32) + leading.astype(
        jnp.float32
    )[:, None] * carried.astype(jnp.float32)
    return (hidden.astype(jnp.float32) + spread).astype(jnp.bfloat16)


def solution(mesh):
    placed = (
        P(("dp", "ctx", "tp"), None),
        P(("dp", "ctx", "tp")),
        P(),
        P(),
        P(),
        P("ctx", "tp"),
        P(),
        P("ctx", "tp"),
        P("ctx", "tp"),
        P("ctx", "tp"),
        P("tp", "ctx"),
        P("tp", "ctx"),
    )
    return jax.shard_map(
        local, mesh=mesh, in_specs=placed, out_specs=P(("dp", "ctx", "tp"), None), check_vma=False
    )
```

profile of v0, /device:TPU:64, one launch (start us, length us, event | category | flops | bytes accessed | tf_op | source)
XLA Modules:
  0.0 502.0 jit_solution(70620909785672022)
XLA Ops:
  11.8 13.8 %all-to-all-start = ((s32[64,1,1]{2,1,0:T(1,128)}), s32[64,1,1]{2,1,0:T(1,128)S(1)}, u32[]{:S(2)}, u32[]{:S(2)}) async-start(s32[64,1,1]{2,1,0:T(1,128)} %broadcast_in_dim.40), calls=%async_computation | async-start | bytes 65536 | tf_op jit(solution)/shard_map/all_to_all | solution.py:27
  26.8 4.9 convolution_convert_fusion.1
  40.6 7.6 %collective-permute-start.5 = (f32[1]{0:T(128)}, f32[1]{0:T(128)}, u32[]{:S(2)}, u32[]{:S(2)}) collective-permute-start(f32[1]{0:T(128)} %bitcast.15), channel_id=1, source_target_pairs={{4,0},{8,4},{12,8},{16,12},{20,16},{24,20},{28,24},{32,28},{36,32}... | collective-permute-start | bytes 20 | tf_op jit(solution)/shard_map/ppermute | solution.py:16
  57.2 22.2 %collective-permute-done.2 = bf16[256,1024]{1,0:T(8,128)(2,1)} collective-permute-done((bf16[256,1024]{1,0:T(8,128)(2,1)S(1)}, bf16[256,1024]{1,0:T(8,128)(2,1)}, u32[]{:S(2)}, u32[]{:S(2)}) %collective-permute-start.2) | collective-permute-done | bytes 524320 | tf_op jit(solution)/shard_map/ppermute | solution.py:16
  82.8 7.7 %collective-permute-done.1 = bf16[256,1024]{1,0:T(8,128)(2,1)S(1)} collective-permute-done((bf16[256,1024]{1,0:T(8,128)(2,1)}, bf16[256,1024]{1,0:T(8,128)(2,1)S(1)}, u32[]{:S(2)}, u32[]{:S(2)}) %collective-permute-start.1) | collective-permute-done | bytes 524320 | tf_op jit(solution)/shard_map/ppermute | solution.py:16
  95.6 5.0 collective-permute-done.3
  105.7 8.4 %fusion.75 = (f32[16,256]{1,0:T(8,128)S(1)}, bf16[16,256,768]{2,1,0:T(8,128)(2,1)}) fusion(pred[256,768]{1,0:T(8,128)(4,1)S(1)} %and_and_fusion, bf16[256,16,64]{0,2,1:T(8,128)(2,1)S(1)} %bitcast.98, bf16[768,16,64]{0,2,1:T(8,128)(2,1)} %bitcast.94), kind=kOutput, calls=%fused_computation.127 | convolution fusion | flops 421528320 | bytes 8601600 | tf_op jit(solution)/shard_map/sub | solution.py:93
  114.1 5.3 %fusion.33 = bf16[256,16,64]{0,2,1:T(8,128)(2,1)S(1)} fusion(bf16[768,16,64]{0,2,1:T(8,128)(2,1)} %bitcast.95, bf16[16,256,768]{2,1,0:T(8,128)(2,1)} %get-tuple-element.30, f32[256,16]{0,1:T(8,128)S(1)} %bitcast.111), kind=kOutput, calls=%fused_computation.41 | convolution fusion | flops 403177472 | bytes 8404992 | tf_op jit(solution)/shard_map/hqk,khd->hqd/dot_general | solution.py:96
  126.3 10.8 %all_to_all.31 = bf16[4,64,1025]{2,1,0:T(8,128)(2,1)S(1)} all-to-all(bf16[4,64,1025]{2,1,0:T(8,128)(2,1)S(1)} %pad_maximum_fusion.2), channel_id=1, replica_groups=mesh['ctx'=16,'tp'=4,'dp'=4] {'tp'}, dimensions={0} | all-to-all | bytes 1049600 | tf_op jit(solution)/shard_map/all_to_all | solution.py:41
  137.5 10.5 %all_to_all.32 = bf16[4,64,1024]{2,1,0:T(8,128)(2,1)S(1)} all-to-all(bf16[4,64,1024]{2,1,0:T(8,128)(2,1)S(1)} %broadcast_in_dim.42), channel_id=1, replica_groups=mesh['ctx'=16,'tp'=4,'dp'=4] {'tp'}, dimensions={0} | all-to-all | bytes 1048576 | tf_op jit(solution)/shard_map/all_to_all | solution.py:27
  150.7 25.1 %all_to_all.33 = bf16[4,256,1024]{1,2,0:T(8,128)(2,1)S(1)} all-to-all(bf16[4,256,1024]{1,2,0:T(8,128)(2,1)S(1)} %broadcast_in_dim.43), channel_id=1, replica_groups=mesh['ctx'=16,'tp'=4,'dp'=4] {'tp'}, dimensions={0} | all-to-all | bytes 4194304 | tf_op jit(solution)/shard_map/all_to_all | solution.py:27
  178.0 46.4 %all-gather.8.cloned.1.call-done = bf16[4096,768]{1,0:T(8,128)(2,1)} async-done(((bf16[256,768]{1,0:T(8,128)(2,1)}), bf16[4096,768]{1,0:T(8,128)(2,1)}) %all-gather.8.cloned.1.call-update) | async-done | bytes 6291472 | tf_op jit(solution)/shard_map/all_gather | solution.py:62
  232.7 4.3 compare_select_fusion.1
  237.0 5.6 %fusion.63 = pred[4096]{0:T(1024)(128)(4,1)S(1)} fusion(pred[4096]{0:T(1024)(128)(4,1)S(1)} %compare_reduce_fusion, pred[4096]{0:T(1024)(128)(4,1)S(1)} %compare_reduce_fusion.1, pred[4096]{0:T(1024)(128)(4,1)S(1)} %compare_reduce_fusion.2, pred[4096]{0:T(1024)(128)(4,1)S(1)} %compare_reduce_fusion.3, pred[4096]{0:T(1024)(128)(4,1)S(1)} %compare_reduce_fusion.4, ...), kind=kLoop, calls=%fused_computation.96 | loop fusion | flops 65536 | bytes 57380 | tf_op jit(solution)/shard_map/lt | solution.py:199
  246.2 60.9 %all-gather.10.cloned.1.call-done = bf16[4096,256]{0,1:T(8,128)(2,1)} async-done(((bf16[256,256]{0,1:T(8,128)(2,1)}), bf16[4096,256]{0,1:T(8,128)(2,1)}) %all-gather.10.cloned.1.call-update) | async-done | bytes 2097168 | tf_op jit(solution)/shard_map/all_gather | solution.py:62
  307.1 6.7 %fusion.2 = (f32[1024]{0:T(1024)S(1)}, f32[1024,4096]{1,0:T(8,128)S(1)}) fusion(s32[1024]{0:T(1024)S(1)} %bitcast.105, pred[4096]{0:T(1024)(128)(4,1)S(1)} %fusion.63, bf16[1024,128]{1,0:T(8,128)(2,1)S(1)} %bitcast.102, bf16[4096,256]{0,1:T(8,128)(2,1)} %all-gather.10.cloned.1.call-done), kind=kOutput, calls=%fused_computation.5 | convolution fusion | flops 1094712320 | bytes 18100224 | tf_op jit(solution)/shard_map/hqd,hkd->hqk/dot_general | solution.py:202
  313.8 7.7 %fusion.70 = f32[1024]{0:T(1024)S(1)} fusion(f32[1024]{0:T(1024)S(1)} %broadcast_maximum_fusion, f32[1024,4096]{1,0:T(8,128)S(1)} %get-tuple-element.32, s32[1024]{0:T(1024)S(1)} %bitcast.106, pred[4096]{0:T(1024)(128)(4,1)S(1)} %fusion.63), kind=kLoop, calls=%fused_computation.123 | loop fusion | flops 29359104 | bytes 16793600 | tf_op jit(solution)/shard_map/reduce_sum | solution.py:207
  321.5 6.0 %fusion.24 = bf16[1024,128]{1,0:T(8,128)(2,1)S(1)} fusion(bf16[4096,256]{0,1:T(8,128)(2,1)S(1)} %copy-done.7, f32[1024]{0:T(1024)S(1)} %fusion.70, f32[1024,4096]{1,0:T(8,128)S(1)} %get-tuple-element.32, f32[1024]{0:T(1024)S(1)} %broadcast_maximum_fusion, s32[1024]{0:T(1024)S(1)} %bitcast.107, pred[4096]{0:T(1024)(128)(4,1)S(1)} %fusion.63), kind=kOutput, calls=%fused_computation.37 | convolution fusion | flops 1103364096 | bytes 18104320 | tf_op jit(solution)/shard_map/hqk,hkd->hqd/dot_general | solution.py:208
  327.6 61.0 %all-gather.12.cloned.1.call-done = bf16[512,4096]{1,0:T(8,128)(2,1)} async-done(((bf16[512,256]{1,0:T(8,128)(2,1)}), bf16[512,4096]{1,0:T(8,128)(2,1)}) %all-gather.12.cloned.1.call-update) | async-done | bytes 4194320 | tf_op jit(solution)/shard_map/all_gather | solution.py:220
  392.2 27.1 %all_to_all.34 = bf16[4,256,1024]{2,1,0:T(8,128)(2,1)S(1)} all-to-all(bf16[4,256,1024]{2,1,0:T(8,128)(2,1)S(1)} %bitcast.93), channel_id=1, replica_groups=mesh['ctx'=16,'tp'=4,'dp'=4] {'tp'}, dimensions={0} | all-to-all | bytes 4194304 | tf_op jit(solution)/shard_map/all_to_all | solution.py:41
  419.8 28.2 %all-gather.14.cloned.1.call-done = bf16[1024,1024]{0,1:T(8,128)(2,1)} async-done(((bf16[1024,64]{0,1:T(8,128)(2,1)}), bf16[1024,1024]{0,1:T(8,128)(2,1)}) %all-gather.14.cloned.1.call-update) | async-done | bytes 2097168 | tf_op jit(solution)/shard_map/all_gather | solution.py:227
  452.0 4.4 all-to-all-start.5
  456.4 25.2 %all-to-all-done.5 = bf16[4,256,1024]{2,1,0:T(8,128)(2,1)} async-done(((bf16[4,256,1024]{2,1,0:T(8,128)(2,1)}), bf16[4,256,1024]{2,1,0:T(8,128)(2,1)}, u32[]{:S(2)}, u32[]{:S(2)}) %all-to-all-start.5) | async-done | bytes 2097184 | tf_op jit(solution)/shard_map/all_to_all | solution.py:27
  486.2 8.1 %collective-permute-done.6 = bf16[1,1024]{1,0:T(2,128)(2,1)S(1)} collective-permute-done((bf16[1,1024]{1,0:T(2,128)(2,1)S(1)}, bf16[1,1024]{1,0:T(2,128)(2,1)S(1)}, u32[]{:S(2)}, u32[]{:S(2)}) %collective-permute-start.6) | collective-permute-done | bytes 2080 | tf_op jit(solution)/shard_map/ppermute | solution.py:16
  (116 shorter events, 73.4 us)
Async XLA Ops:
  6.5 112.9 %copy-start = (bf16[1024,1024]{1,0:T(8,128)(2,1)S(1)}, bf16[1024,1024]{1,0:T(8,128)(2,1)}, u32[]{:S(2)}) copy-start(bf16[1024,1024]{1,0:T(8,128)(2,1)} %param.16) | copy-start | bytes 6291460
  6.5 141.5 %all-gather.6.cloned.1.call-start = ((), (), s32[]{:S(2)}) async-start(), calls=%async_computation.6 | async-start | bytes 2228224 | tf_op jit(solution)/shard_map/all_gather | solution.py:171
  7.3 217.2 %all-gather.8.cloned.1.call-start = ((), (), s32[]{:S(2)}) async-start(), calls=%async_computation.7 | async-start | bytes 6684672 | tf_op jit(solution)/shard_map/all_gather | solution.py:62
  11.8 37.8 %all-to-all-start = ((s32[64,1,1]{2,1,0:T(1,128)}), s32[64,1,1]{2,1,0:T(1,128)S(1)}, u32[]{:S(2)}, u32[]{:S(2)}) async-start(s32[64,1,1]{2,1,0:T(1,128)} %broadcast_in_dim.40), calls=%async_computation | async-start | bytes 65536 | tf_op jit(solution)/shard_map/all_to_all | solution.py:27
  25.5 281.5 %all-gather.10.cloned.1.call-start = ((), (), s32[]{:S(2)}) async-start(), calls=%async_computation.8 | async-start | bytes 2228224 | tf_op jit(solution)/shard_map/all_gather | solution.py:62
  26.8 12.5 %copy-start.6 = (s32[256]{0:T(256)S(1)}, s32[256]{0:T(256)}, u32[]{:S(2)}) copy-start(s32[256]{0:T(256)} %param.13) | copy-start | bytes 3076
  32.6 22.6 %collective-permute-start = (bf16[256,1024]{1,0:T(8,128)(2,1)}, bf16[256,1024]{1,0:T(8,128)(2,1)}, u32[]{:S(2)}, u32[]{:S(2)}) collective-permute-start(bf16[256,1024]{1,0:T(8,128)(2,1)} %get-tuple-element.8), channel_id=1, source_target_pairs={{0,4},{4,8},{8,12},{12,16},{16,20},{20,24},{24,28},{28,32},{32,36}... | collective-permute-start | bytes 1572872 | tf_op jit(solution)/shard_map/ppermute | solution.py:16
  36.0 43.4 %collective-permute-start.2 = (bf16[256,1024]{1,0:T(8,128)(2,1)S(1)}, bf16[256,1024]{1,0:T(8,128)(2,1)}, u32[]{:S(2)}, u32[]{:S(2)}) collective-permute-start(bf16[256,1024]{1,0:T(8,128)(2,1)S(1)} %get-tuple-element.9), channel_id=1, source_target_pairs={{0,4},{4,8},{8,12},{12,16},{16,20},{20,24},{24,28},{28,32},{32,36}... | collective-permute-start | bytes 1572872 | tf_op jit(solution)/shard_map/ppermute | solution.py:16
  40.6 41.6 %collective-permute-start.5 = (f32[1]{0:T(128)}, f32[1]{0:T(128)}, u32[]{:S(2)}, u32[]{:S(2)}) collective-permute-start(f32[1]{0:T(128)} %bitcast.15), channel_id=1, source_target_pairs={{4,0},{8,4},{12,8},{16,12},{20,16},{24,20},{28,24},{32,28},{36,32}... | collective-permute-start | bytes 20 | tf_op jit(solution)/shard_map/ppermute | solution.py:16
  55.2 35.3 %collective-permute-start.1 = (bf16[256,1024]{1,0:T(8,128)(2,1)}, bf16[256,1024]{1,0:T(8,128)(2,1)S(1)}, u32[]{:S(2)}, u32[]{:S(2)}) collective-permute-start(bf16[256,1024]{1,0:T(8,128)(2,1)} %collective-permute-done), channel_id=1, source_target_pairs={{0,4},{4,8},{8,12},{12,16},{16,20},{20,24},{24,28},{28,32},{32,36}... | collective-permute-start | bytes 1572872 | tf_op jit(solution)/shard_map/ppermute | solution.py:16
  79.4 21.2 %collective-permute-start.3 = (bf16[256,1024]{1,0:T(8,128)(2,1)}, bf16[256,1024]{1,0:T(8,128)(2,1)}, u32[]{:S(2)}, u32[]{:S(2)}) collective-permute-start(bf16[256,1024]{1,0:T(8,128)(2,1)} %collective-permute-done.2), channel_id=1, source_target_pairs={{0,4},{4,8},{8,12},{12,16},{16,20},{20,24},{24,28},{28,32},{32,36}... | collective-permute-start | bytes 1572872 | tf_op jit(solution)/shard_map/ppermute | solution.py:16
  93.0 12.7 %copy-start.4 = (bf16[256,1024]{0,1:T(8,128)(2,1)S(1)}, bf16[256,1024]{0,1:T(8,128)(2,1)}, u32[]{:S(2)}) copy-start(bf16[256,1024]{0,1:T(8,128)(2,1)} %copy.45) | copy-start | bytes 1572868
  114.1 5.3 %copy-start.3 = (bf16[256,1024]{1,0:T(8,128)(2,1)S(1)}, bf16[256,1024]{1,0:T(8,128)(2,1)}, u32[]{:S(2)}) copy-start(bf16[256,1024]{1,0:T(8,128)(2,1)} %param.12) | copy-start | bytes 1572868
  120.3 5.5 %collective-permute-start.4 = (f32[1,1024]{1,0:T(1,128)S(1)}, f32[1,1024]{1,0:T(1,128)S(1)}, u32[]{:S(2)}, u32[]{:S(2)}) collective-permute-start(f32[1,1024]{1,0:T(1,128)S(1)} %fusion.76), channel_id=1, source_target_pairs={{4,0},{8,4},{12,8},{16,12},{20,16},{24,20},{28,24},{32,28},{36,32}... | collective-permute-start | bytes 12296 | tf_op jit(solution)/shard_map/ppermute | solution.py:16
  150.5 25.8 %copy-start.5 = (f32[4096]{0:T(1024)S(1)}, f32[4096]{0:T(1024)}, u32[]{:S(2)}) copy-start(f32[4096]{0:T(1024)} %param.18) | copy-start | bytes 49156
  178.0 64.6 %copy-start.2 = (bf16[256,4096]{0,1:T(8,128)(2,1)S(1)}, bf16[256,4096]{0,1:T(8,128)(2,1)}, u32[]{:S(2)}) copy-start(bf16[256,4096]{0,1:T(8,128)(2,1)} %fusion.14) | copy-start | bytes 6291460
  230.0 158.6 %all-gather.12.cloned.1.call-start = ((), (), s32[]{:S(2)}) async-start(), calls=%async_computation.9 | async-start | bytes 4456448 | tf_op jit(solution)/shard_map/all_gather | solution.py:220
  230.6 217.4 %all-gather.14.cloned.1.call-start = ((), (), s32[]{:S(2)}) async-start(), calls=%async_computation.10 | async-start | bytes 2228224 | tf_op jit(solution)/shard_map/all_gather | solution.py:227
  313.8 7.7 %copy-start.7 = (bf16[4096,256]{0,1:T(8,128)(2,1)S(1)}, bf16[4096,256]{0,1:T(8,128)(2,1)}, u32[]{:S(2)}) copy-start(bf16[4096,256]{0,1:T(8,128)(2,1)} %all-gather.10.cloned.1.call-done) | copy-start | bytes 6291460
  450.4 45.1 %copy-start.1 = (bf16[1024,1024]{1,0:T(8,128)(2,1)S(1)}, bf16[1024,1024]{1,0:T(8,128)(2,1)}, u32[]{:S(2)}) copy-start(bf16[1024,1024]{1,0:T(8,128)(2,1)} %param.16) | copy-start | bytes 6291460
  452.0 29.7 %all-to-all-start.5 = ((bf16[4,256,1024]{2,1,0:T(8,128)(2,1)}), bf16[4,256,1024]{2,1,0:T(8,128)(2,1)}, u32[]{:S(2)}, u32[]{:S(2)}) async-start(bf16[4,256,1024]{2,1,0:T(8,128)(2,1)} %broadcast_in_dim.82), calls=%async_computation.5 | async-start | bytes 4194304 | tf_op jit(solution)/shard_map/all_to_all | solution.py:27
  483.7 10.6 %collective-permute-start.6 = (bf16[1,1024]{1,0:T(2,128)(2,1)S(1)}, bf16[1,1024]{1,0:T(2,128)(2,1)S(1)}, u32[]{:S(2)}, u32[]{:S(2)}) collective-permute-start(bf16[1,1024]{1,0:T(2,128)(2,1)S(1)} %constant_dynamic-slice_fusion), channel_id=1, source_target_pairs={{0,4},{4,8},{8,12},{12,16},{16,20},{20,24},{24,28},{28,32},{32,36}... | collective-permute-start | bytes 6152 | tf_op jit(solution)/shard_map/ppermute | solution.py:16
Sparse Core Ops, SparseCore 0:
  9.8 61.1 all-gather.5
  73.4 151.0 all-gather.7
  230.1 76.9 all-gather.9
  309.3 79.2 all-gather.11
  390.9 57.1 all-gather.13
where the time goes:
time: 503 us; the launch traced here: 502 us
  waiting for transfers between devices  272 us (54%)
  blocking collectives  73.5 us (15%)
  matrix products  50.1 us (10%)
  starting transfers between devices  40.9 us (8%)
  other arithmetic  36.8 us (7%)
  between operations  15.6 us (3%)
  local copies, waits for them, and re-layouts  12.8 us (3%)
    all_gather x2, waiting for transfers between devices, sent_together(): lax.all_gather(both, axis, axis=dim, tiled=True)  107 us
    all_gather x1, waiting for transfers between devices, local(): lax.all_gather(out_proj, 'ctx', axis=1, tiled=True)  61 us
    ppermute x7, waiting for transfers between devices, shifted(): return lax.ppermute(block, axis, route)  48.8 us
    all_to_all x2, blocking collectives, sum_at_owner(): lax.all_to_all(parts, axis, split_axis=0, concat_axis=0, tiled=True)  38 us
    all_to_all x2, blocking collectives, from_everyone(): return lax.all_to_all(copies, axis, split_axis=0, concat_axis=0, tiled=True)  35.6 us
    all_gather x1, waiting for transfers between devices, local(): lax.all_gather(down_proj, 'ctx', axis=1, tiled=True)  28.2 us
    all_to_all x2, waiting for transfers between devices, from_everyone(): return lax.all_to_all(copies, axis, split_axis=0, concat_axis=0, tiled=True)  25.2 us
    ppermute x7, starting transfers between devices, shifted(): return lax.ppermute(block, axis, route)  22.5 us
  transfers between devices with their start and end apart: 14, of which 11 were waited for; matrix products, arithmetic and copies ran while one was open for 17% of the time, Pallas kernels for 0%

commit v1 on v0

--- a/solution.py
+++ b/solution.py
@@ -217,7 +217,9 @@
     )
     partial_value = jnp.dot(
         attn,
-        lax.all_gather(out_proj, "ctx", axis=1, tiled=True),
+        jnp.concatenate(
+            lax.all_to_all(jnp.stack([out_proj] * lax.axis_size("ctx")), "ctx", 0, 0), axis=1
+        ),
         preferred_element_type=jnp.float32,
     )
     attn_part = sum_at_owner(partial_value.astype(jnp.bfloat16), "tp", 1)

time: 503 us -> 481 us (0.956)
  waiting for transfers between devices: 272 us -> 236 us
  starting transfers between devices: 40.9 us -> 47.9 us
    all_gather x1 -> x0, waiting for transfers between devices: 61 us -> none  [local(): lax.all_gather(out_proj, 'ctx', axis=1, tiled=True)]
    all_gather x2, waiting for transfers between devices: 107 us -> 153 us  [sent_together(): lax.all_gather(both, axis, axis=dim, tiled=True)]
    all_gather x1, waiting for transfers between devices: 28.2 us -> 7.56 us  [local(): lax.all_gather(down_proj, 'ctx', axis=1, tiled=True)]
    all_to_all x0 -> x1, starting transfers between devices: none -> 7.06 us  [local(): lax.all_to_all(jnp.stack([out_proj] * lax.axis_size('ctx')), 'ctx', 0, 0)]
  transfers between devices with their start and end apart: 14 -> 14, of which waited for: 11 -> 10; matrix products, arithmetic and copies ran while one was open for 17% -> 19% of each run, Pallas kernels for 0% -> 0%
where the time goes in v1:
time: 481 us; the launch traced here: 479 us
  waiting for transfers between devices  236 us (49%)
  blocking collectives  77.5 us (16%)
  matrix products  50.1 us (10%)
  starting transfers between devices  47.9 us (10%)
  other arithmetic  36.9 us (8%)
  between operations  15.6 us (3%)
  local copies, waits for them, and re-layouts  15.4 us (3%)
    all_gather x2, waiting for transfers between devices, sent_together(): lax.all_gather(both, axis, axis=dim, tiled=True)  153 us
    ppermute x7, waiting for transfers between devices, shifted(): return lax.ppermute(block, axis, route)  48.8 us
    all_to_all x2, blocking collectives, sum_at_owner(): lax.all_to_all(parts, axis, split_axis=0, concat_axis=0, tiled=True)  42 us
    all_to_all x2, blocking collectives, from_everyone(): return lax.all_to_all(copies, axis, split_axis=0, concat_axis=0, tiled=True)  35.6 us
    all_to_all x2, waiting for transfers between devices, from_everyone(): return lax.all_to_all(copies, axis, split_axis=0, concat_axis=0, tiled=True)  25.1 us
    ppermute x7, starting transfers between devices, shifted(): return lax.ppermute(block, axis, route)  22.5 us
    all_to_all x2, starting transfers between devices, from_everyone(): return lax.all_to_all(copies, axis, split_axis=0, concat_axis=0, tiled=True)  18.2 us
  transfers between devices with their start and end apart: 14, of which 10 were waited for; matrix products, arithmetic and copies ran while one was open for 19% of the time, Pallas kernels for 0%

profile of v1, /device:TPU:64, one launch (start us, length us, event | category | flops | bytes accessed | tf_op | source)
XLA Modules:
  0.0 479.2 jit_solution(5023694886515261013)
XLA Ops:
  11.8 13.8 %all-to-all-start = ((s32[64,1,1]{2,1,0:T(1,128)}), s32[64,1,1]{2,1,0:T(1,128)S(1)}, u32[]{:S(2)}, u32[]{:S(2)}) async-start(s32[64,1,1]{2,1,0:T(1,128)} %broadcast_in_dim.40), calls=%async_computation | async-start | bytes 65536 | tf_op jit(solution)/shard_map/all_to_all | solution.py:27
  26.8 4.9 %convolution_convert_fusion.1 = bf16[256,3072]{1,0:T(8,128)(2,1)S(1)} fusion(bf16[1024,3072]{1,0:T(8,128)(2,1)} %param.15, bf16[256,1024]{1,0:T(8,128)(2,1)} %param.12, f32[1024]{0:T(1024)} %param.14, f32[256]{0:T(256)S(1)} %add_rsqrt_fusion.1), kind=kOutput, calls=%fused_computation.24 | convolution fusion | flops 1612447744 | bytes 8393728 | tf_op jit(solution)/shard_map/dot_general | solution.py:126
  40.6 7.6 %collective-permute-start.5 = (f32[1]{0:T(128)}, f32[1]{0:T(128)}, u32[]{:S(2)}, u32[]{:S(2)}) collective-permute-start(f32[1]{0:T(128)} %bitcast.15), channel_id=1, source_target_pairs={{4,0},{8,4},{12,8},{16,12},{20,16},{24,20},{28,24},{32,28},{36,32}... | collective-permute-start | bytes 20 | tf_op jit(solution)/shard_map/ppermute | solution.py:16
  57.2 22.2 %collective-permute-done.2 = bf16[256,1024]{1,0:T(8,128)(2,1)} collective-permute-done((bf16[256,1024]{1,0:T(8,128)(2,1)S(1)}, bf16[256,1024]{1,0:T(8,128)(2,1)}, u32[]{:S(2)}, u32[]{:S(2)}) %collective-permute-start.2) | collective-permute-done | bytes 524320 | tf_op jit(solution)/shard_map/ppermute | solution.py:16
  82.8 7.7 %collective-permute-done.1 = bf16[256,1024]{1,0:T(8,128)(2,1)S(1)} collective-permute-done((bf16[256,1024]{1,0:T(8,128)(2,1)}, bf16[256,1024]{1,0:T(8,128)(2,1)S(1)}, u32[]{:S(2)}, u32[]{:S(2)}) %collective-permute-start.1) | collective-permute-done | bytes 524320 | tf_op jit(solution)/shard_map/ppermute | solution.py:16
  95.6 5.0 %collective-permute-done.3 = bf16[256,1024]{1,0:T(8,128)(2,1)} collective-permute-done((bf16[256,1024]{1,0:T(8,128)(2,1)}, bf16[256,1024]{1,0:T(8,128)(2,1)}, u32[]{:S(2)}, u32[]{:S(2)}) %collective-permute-start.3) | collective-permute-done | bytes 524320 | tf_op jit(solution)/shard_map/ppermute | solution.py:16
  105.7 8.4 %fusion.75 = (f32[16,256]{1,0:T(8,128)S(1)}, bf16[16,256,768]{2,1,0:T(8,128)(2,1)}) fusion(pred[256,768]{1,0:T(8,128)(4,1)S(1)} %and_and_fusion, bf16[256,16,64]{0,2,1:T(8,128)(2,1)S(1)} %bitcast.101, bf16[768,16,64]{0,2,1:T(8,128)(2,1)} %bitcast.97), kind=kOutput, calls=%fused_computation.127 | convolution fusion | flops 421528320 | bytes 8601600 | tf_op jit(solution)/shard_map/sub | solution.py:93
  114.1 5.3 %fusion.33 = bf16[256,16,64]{0,2,1:T(8,128)(2,1)S(1)} fusion(bf16[768,16,64]{0,2,1:T(8,128)(2,1)} %bitcast.98, bf16[16,256,768]{2,1,0:T(8,128)(2,1)} %get-tuple-element.30, f32[256,16]{0,1:T(8,128)S(1)} %bitcast.114), kind=kOutput, calls=%fused_computation.41 | convolution fusion | flops 403177472 | bytes 8404992 | tf_op jit(solution)/shard_map/hqk,khd->hqd/dot_general | solution.py:96
  126.3 10.8 %all_to_all.36 = bf16[4,64,1025]{2,1,0:T(8,128)(2,1)S(1)} all-to-all(bf16[4,64,1025]{2,1,0:T(8,128)(2,1)S(1)} %pad_maximum_fusion.2), channel_id=1, replica_groups=mesh['ctx'=16,'tp'=4,'dp'=4] {'tp'}, dimensions={0} | all-to-all | bytes 1049600 | tf_op jit(solution)/shard_map/all_to_all | solution.py:41
  137.5 10.5 %all_to_all.37 = bf16[4,64,1024]{2,1,0:T(8,128)(2,1)S(1)} all-to-all(bf16[4,64,1024]{2,1,0:T(8,128)(2,1)S(1)} %broadcast_in_dim.42), channel_id=1, replica_groups=mesh['ctx'=16,'tp'=4,'dp'=4] {'tp'}, dimensions={0} | all-to-all | bytes 1048576 | tf_op jit(solution)/shard_map/all_to_all | solution.py:27
  150.7 25.1 %all_to_all.38 = bf16[4,256,1024]{1,2,0:T(8,128)(2,1)S(1)} all-to-all(bf16[4,256,1024]{1,2,0:T(8,128)(2,1)S(1)} %broadcast_in_dim.43), channel_id=1, replica_groups=mesh['ctx'=16,'tp'=4,'dp'=4] {'tp'}, dimensions={0} | all-to-all | bytes 4194304 | tf_op jit(solution)/shard_map/all_to_all | solution.py:27
  178.0 46.5 %all-gather.7.cloned.1.call-done = bf16[4096,768]{1,0:T(8,128)(2,1)} async-done(((bf16[256,768]{1,0:T(8,128)(2,1)}), bf16[4096,768]{1,0:T(8,128)(2,1)}) %all-gather.7.cloned.1.call-update) | async-done | bytes 6291472 | tf_op jit(solution)/shard_map/all_gather | solution.py:62
  232.7 7.1 %all-to-all-start.4 = ((bf16[16,512,256]{1,2,0:T(8,128)(2,1)}), bf16[16,512,256]{1,2,0:T(8,128)(2,1)}, u32[]{:S(2)}, u32[]{:S(2)}) async-start(bf16[16,512,256]{1,2,0:T(8,128)(2,1)} %stack.2), calls=%async_computation.4 | async-start | bytes 8388608 | tf_op jit(solution)/shard_map/all_to_all | solution.py:221
  241.8 4.5 compare_select_fusion.1
  246.3 5.6 %fusion.63 = pred[4096]{0:T(1024)(128)(4,1)S(1)} fusion(pred[4096]{0:T(1024)(128)(4,1)S(1)} %compare_reduce_fusion, pred[4096]{0:T(1024)(128)(4,1)S(1)} %compare_reduce_fusion.1, pred[4096]{0:T(1024)(128)(4,1)S(1)} %compare_reduce_fusion.2, pred[4096]{0:T(1024)(128)(4,1)S(1)} %compare_reduce_fusion.3, pred[4096]{0:T(1024)(128)(4,1)S(1)} %compare_reduce_fusion.4, ...), kind=kLoop, calls=%fused_computation.96 | loop fusion | flops 65536 | bytes 57380 | tf_op jit(solution)/shard_map/lt | solution.py:199
  255.4 106.6 %all-gather.9.cloned.1.call-done = bf16[4096,256]{0,1:T(8,128)(2,1)} async-done(((bf16[256,256]{0,1:T(8,128)(2,1)}), bf16[4096,256]{0,1:T(8,128)(2,1)}) %all-gather.9.cloned.1.call-update) | async-done | bytes 2097168 | tf_op jit(solution)/shard_map/all_gather | solution.py:62
  362.0 6.7 %fusion.2 = (f32[1024]{0:T(1024)S(1)}, f32[1024,4096]{1,0:T(8,128)S(1)}) fusion(s32[1024]{0:T(1024)S(1)} %bitcast.108, pred[4096]{0:T(1024)(128)(4,1)S(1)} %fusion.63, bf16[1024,128]{1,0:T(8,128)(2,1)S(1)} %bitcast.105, bf16[4096,256]{0,1:T(8,128)(2,1)} %all-gather.9.cloned.1.call-done), kind=kOutput, calls=%fused_computation.5 | convolution fusion | flops 1094712320 | bytes 18100224 | tf_op jit(solution)/shard_map/hqd,hkd->hqk/dot_general | solution.py:202
  368.7 7.7 %fusion.70 = f32[1024]{0:T(1024)S(1)} fusion(f32[1024]{0:T(1024)S(1)} %broadcast_maximum_fusion, f32[1024,4096]{1,0:T(8,128)S(1)} %get-tuple-element.32, s32[1024]{0:T(1024)S(1)} %bitcast.109, pred[4096]{0:T(1024)(128)(4,1)S(1)} %fusion.63), kind=kLoop, calls=%fused_computation.123 | loop fusion | flops 29359104 | bytes 16793600 | tf_op jit(solution)/shard_map/reduce_sum | solution.py:207
  376.4 6.0 %fusion.24 = bf16[1024,128]{1,0:T(8,128)(2,1)S(1)} fusion(bf16[4096,256]{0,1:T(8,128)(2,1)S(1)} %copy-done.8, f32[1024]{0:T(1024)S(1)} %fusion.70, f32[1024,4096]{1,0:T(8,128)S(1)} %get-tuple-element.32, f32[1024]{0:T(1024)S(1)} %broadcast_maximum_fusion, s32[1024]{0:T(1024)S(1)} %bitcast.110, pred[4096]{0:T(1024)(128)(4,1)S(1)} %fusion.63), kind=kOutput, calls=%fused_computation.37 | convolution fusion | flops 1103364096 | bytes 18104320 | tf_op jit(solution)/shard_map/hqk,hkd->hqd/dot_general | solution.py:208
  386.3 31.2 %all_to_all.39 = bf16[4,256,1024]{2,1,0:T(8,128)(2,1)S(1)} all-to-all(bf16[4,256,1024]{2,1,0:T(8,128)(2,1)S(1)} %bitcast.96), channel_id=1, replica_groups=mesh['ctx'=16,'tp'=4,'dp'=4] {'tp'}, dimensions={0} | all-to-all | bytes 4194304 | tf_op jit(solution)/shard_map/all_to_all | solution.py:41
  417.8 7.6 %all-gather.11.cloned.1.call-done = bf16[1024,1024]{0,1:T(8,128)(2,1)} async-done(((bf16[1024,64]{0,1:T(8,128)(2,1)}), bf16[1024,1024]{0,1:T(8,128)(2,1)}) %all-gather.11.cloned.1.call-update) | async-done | bytes 2097168 | tf_op jit(solution)/shard_map/all_gather | solution.py:229
  429.3 4.4 all-to-all-start.6
  433.8 25.1 %all-to-all-done.6 = bf16[4,256,1024]{2,1,0:T(8,128)(2,1)} async-done(((bf16[4,256,1024]{2,1,0:T(8,128)(2,1)}), bf16[4,256,1024]{2,1,0:T(8,128)(2,1)}, u32[]{:S(2)}, u32[]{:S(2)}) %all-to-all-start.6) | async-done | bytes 2097184 | tf_op jit(solution)/shard_map/all_to_all | solution.py:27
  463.4 8.1 %collective-permute-done.6 = bf16[1,1024]{1,0:T(2,128)(2,1)S(1)} collective-permute-done((bf16[1,1024]{1,0:T(2,128)(2,1)S(1)}, bf16[1,1024]{1,0:T(2,128)(2,1)S(1)}, u32[]{:S(2)}, u32[]{:S(2)}) %collective-permute-start.6) | collective-permute-done | bytes 2080 | tf_op jit(solution)/shard_map/ppermute | solution.py:16
  (119 shorter events, 75.5 us)
Async XLA Ops:
  6.5 112.9 %copy-start = (bf16[1024,1024]{1,0:T(8,128)(2,1)S(1)}, bf16[1024,1024]{1,0:T(8,128)(2,1)}, u32[]{:S(2)}) copy-start(bf16[1024,1024]{1,0:T(8,128)(2,1)} %param.16) | copy-start | bytes 6291460
  6.5 141.5 %all-gather.5.cloned.1.call-start = ((), (), s32[]{:S(2)}) async-start(), calls=%async_computation.7 | async-start | bytes 2228224 | tf_op jit(solution)/shard_map/all_gather | solution.py:171
  7.3 217.2 %all-gather.7.cloned.1.call-start = ((), (), s32[]{:S(2)}) async-start(), calls=%async_computation.8 | async-start | bytes 6684672 | tf_op jit(solution)/shard_map/all_gather | solution.py:62
  11.8 37.8 %all-to-all-start = ((s32[64,1,1]{2,1,0:T(1,128)}), s32[64,1,1]{2,1,0:T(1,128)S(1)}, u32[]{:S(2)}, u32[]{:S(2)}) async-start(s32[64,1,1]{2,1,0:T(1,128)} %broadcast_in_dim.40), calls=%async_computation | async-start | bytes 65536 | tf_op jit(solution)/shard_map/all_to_all | solution.py:27
  25.5 336.4 %all-gather.9.cloned.1.call-start = ((), (), s32[]{:S(2)}) async-start(), calls=%async_computation.9 | async-start | bytes 2228224 | tf_op jit(solution)/shard_map/all_gather | solution.py:62
  26.8 12.5 %copy-start.7 = (s32[256]{0:T(256)S(1)}, s32[256]{0:T(256)}, u32[]{:S(2)}) copy-start(s32[256]{0:T(256)} %param.13) | copy-start | bytes 3076
  32.6 22.6 %collective-permute-start = (bf16[256,1024]{1,0:T(8,128)(2,1)}, bf16[256,1024]{1,0:T(8,128)(2,1)}, u32[]{:S(2)}, u32[]{:S(2)}) collective-permute-start(bf16[256,1024]{1,0:T(8,128)(2,1)} %get-tuple-element.8), channel_id=1, source_target_pairs={{0,4},{4,8},{8,12},{12,16},{16,20},{20,24},{24,28},{28,32},{32,36}... | collective-permute-start | bytes 1572872 | tf_op jit(solution)/shard_map/ppermute | solution.py:16
  36.0 43.4 %collective-permute-start.2 = (bf16[256,1024]{1,0:T(8,128)(2,1)S(1)}, bf16[256,1024]{1,0:T(8,128)(2,1)}, u32[]{:S(2)}, u32[]{:S(2)}) collective-permute-start(bf16[256,1024]{1,0:T(8,128)(2,1)S(1)} %get-tuple-element.9), channel_id=1, source_target_pairs={{0,4},{4,8},{8,12},{12,16},{16,20},{20,24},{24,28},{28,32},{32,36}... | collective-permute-start | bytes 1572872 | tf_op jit(solution)/shard_map/ppermute | solution.py:16
  40.6 41.6 %collective-permute-start.5 = (f32[1]{0:T(128)}, f32[1]{0:T(128)}, u32[]{:S(2)}, u32[]{:S(2)}) collective-permute-start(f32[1]{0:T(128)} %bitcast.15), channel_id=1, source_target_pairs={{4,0},{8,4},{12,8},{16,12},{20,16},{24,20},{28,24},{32,28},{36,32}... | collective-permute-start | bytes 20 | tf_op jit(solution)/shard_map/ppermute | solution.py:16
  55.2 35.3 %collective-permute-start.1 = (bf16[256,1024]{1,0:T(8,128)(2,1)}, bf16[256,1024]{1,0:T(8,128)(2,1)S(1)}, u32[]{:S(2)}, u32[]{:S(2)}) collective-permute-start(bf16[256,1024]{1,0:T(8,128)(2,1)} %collective-permute-done), channel_id=1, source_target_pairs={{0,4},{4,8},{8,12},{12,16},{16,20},{20,24},{24,28},{28,32},{32,36}... | collective-permute-start | bytes 1572872 | tf_op jit(solution)/shard_map/ppermute | solution.py:16
  79.4 21.2 %collective-permute-start.3 = (bf16[256,1024]{1,0:T(8,128)(2,1)}, bf16[256,1024]{1,0:T(8,128)(2,1)}, u32[]{:S(2)}, u32[]{:S(2)}) collective-permute-start(bf16[256,1024]{1,0:T(8,128)(2,1)} %collective-permute-done.2), channel_id=1, source_target_pairs={{0,4},{4,8},{8,12},{12,16},{16,20},{20,24},{24,28},{28,32},{32,36}... | collective-permute-start | bytes 1572872 | tf_op jit(solution)/shard_map/ppermute | solution.py:16
  93.0 12.7 %copy-start.4 = (bf16[256,1024]{0,1:T(8,128)(2,1)S(1)}, bf16[256,1024]{0,1:T(8,128)(2,1)}, u32[]{:S(2)}) copy-start(bf16[256,1024]{0,1:T(8,128)(2,1)} %copy.48) | copy-start | bytes 1572868
  114.1 5.3 %copy-start.3 = (bf16[256,1024]{1,0:T(8,128)(2,1)S(1)}, bf16[256,1024]{1,0:T(8,128)(2,1)}, u32[]{:S(2)}) copy-start(bf16[256,1024]{1,0:T(8,128)(2,1)} %param.12) | copy-start | bytes 1572868
  120.3 5.5 %collective-permute-start.4 = (f32[1,1024]{1,0:T(1,128)S(1)}, f32[1,1024]{1,0:T(1,128)S(1)}, u32[]{:S(2)}, u32[]{:S(2)}) collective-permute-start(f32[1,1024]{1,0:T(1,128)S(1)} %fusion.76), channel_id=1, source_target_pairs={{4,0},{8,4},{12,8},{16,12},{20,16},{24,20},{28,24},{32,28},{36,32}... | collective-permute-start | bytes 12296 | tf_op jit(solution)/shard_map/ppermute | solution.py:16
  150.5 25.8 %copy-start.6 = (f32[4096]{0:T(1024)S(1)}, f32[4096]{0:T(1024)}, u32[]{:S(2)}) copy-start(f32[4096]{0:T(1024)} %param.18) | copy-start | bytes 49156
  178.0 52.0 %copy-start.5 = (bf16[512,256]{1,0:T(8,128)(2,1)S(1)}, bf16[512,256]{1,0:T(8,128)(2,1)}, u32[]{:S(2)}) copy-start(bf16[512,256]{1,0:T(8,128)(2,1)} %param.22) | copy-start | bytes 786436
  232.7 19.2 %copy-start.2 = (bf16[256,4096]{0,1:T(8,128)(2,1)S(1)}, bf16[256,4096]{0,1:T(8,128)(2,1)}, u32[]{:S(2)}) copy-start(bf16[256,4096]{0,1:T(8,128)(2,1)} %fusion.14) | copy-start | bytes 6291460
  232.7 149.9 %all-to-all-start.4 = ((bf16[16,512,256]{1,2,0:T(8,128)(2,1)}), bf16[16,512,256]{1,2,0:T(8,128)(2,1)}, u32[]{:S(2)}, u32[]{:S(2)}) async-start(bf16[16,512,256]{1,2,0:T(8,128)(2,1)} %stack.2), calls=%async_computation.4 | async-start | bytes 8388608 | tf_op jit(solution)/shard_map/all_to_all | solution.py:221
  239.7 185.7 %all-gather.11.cloned.1.call-start = ((), (), s32[]{:S(2)}) async-start(), calls=%async_computation.10 | async-start | bytes 2228224 | tf_op jit(solution)/shard_map/all_gather | solution.py:229
  368.7 7.7 %copy-start.8 = (bf16[4096,256]{0,1:T(8,128)(2,1)S(1)}, bf16[4096,256]{0,1:T(8,128)(2,1)}, u32[]{:S(2)}) copy-start(bf16[4096,256]{0,1:T(8,128)(2,1)} %all-gather.9.cloned.1.call-done) | copy-start | bytes 6291460
  427.7 45.0 %copy-start.1 = (bf16[1024,1024]{1,0:T(8,128)(2,1)S(1)}, bf16[1024,1024]{1,0:T(8,128)(2,1)}, u32[]{:S(2)}) copy-start(bf16[1024,1024]{1,0:T(8,128)(2,1)} %param.16) | copy-start | bytes 6291460
  429.3 29.6 %all-to-all-start.6 = ((bf16[4,256,1024]{2,1,0:T(8,128)(2,1)}), bf16[4,256,1024]{2,1,0:T(8,128)(2,1)}, u32[]{:S(2)}, u32[]{:S(2)}) async-start(bf16[4,256,1024]{2,1,0:T(8,128)(2,1)} %broadcast_in_dim.82), calls=%async_computation.6 | async-start | bytes 4194304 | tf_op jit(solution)/shard_map/all_to_all | solution.py:27
  460.9 10.6 %collective-permute-start.6 = (bf16[1,1024]{1,0:T(2,128)(2,1)S(1)}, bf16[1,1024]{1,0:T(2,128)(2,1)S(1)}, u32[]{:S(2)}, u32[]{:S(2)}) collective-permute-start(bf16[1,1024]{1,0:T(2,128)(2,1)S(1)} %constant_dynamic-slice_fusion), channel_id=1, source_target_pairs={{0,4},{4,8},{8,12},{12,16},{16,20},{20,24},{24,28},{28,32},{32,36}... | collective-permute-start | bytes 6152 | tf_op jit(solution)/shard_map/ppermute | solution.py:16
Sparse Core Ops, SparseCore 0:
  9.8 61.1 all-gather.4
  73.4 151.0 all-gather.6
  230.1 131.8 all-gather.8
  364.3 61.0 all-gather.10
